TPU v7x, 32 devices: a whole 2x2x4 slice. The times are simulated.
32 devices in a mesh: row: 8 (over z, x), col: 4 (over y, core).
Axes of the slice: x: 2, y: 2, z: 4, core: 2. Of those that a mesh axis runs over, the one named last changes fastest.
Arguments:
- tile_values: bfloat16 [192, 512, 128], P('row', 'col'), may hold values from -0.0546875 to 0.0546875
- tile_counts: int32 [96, 4], P('row', 'col'), may hold values from 0 to 2, as said below
- tile_cols: int32 [192, 4], P('row', 'col'), may hold values from 0 to 1, as said below
- panels: bfloat16 [12288, 4096], P('row', 'col'), may hold values from -6 to 6
Outputs:
- product: bfloat16 [1024, 4096], P('col', 'row')
Inputs may be any that keep to these rules, and one draw needn't show every extreme that they name: `tile_counts`: within each device the filled slots follow block row order; a device holds at most 24 tiles and some device holds exactly 24 in every draw. `tile_cols`: within one block row of a device the filled slots' columns rise strictly; entries of unfilled slots carry no meaning.
All inputs are finite; a program needn't handle non-finite values.
Results may differ from a plain program's by a relative error of at most 0.001.
Values may be sent and summed in bfloat16 or wider, within the bound.
A program may use at most 64 MiB of HBM per device.

v0:
```python
import jax
import jax.numpy as jnp
from jax import lax
from jax.sharding import PartitionSpec as P

BC_DEV = 2


def selection(tile_counts, tile_cols, slots, blocks_wide):
    counts = tile_counts[:, 0]
    row_start = jnp.cumsum(counts) - counts
    slot_ids = jnp.arange(slots, dtype=jnp.int32)[:, None]
    row_mask = (slot_ids >= row_start[None, :]) & (slot_ids < (row_start + counts)[None, :])
    col_mask = tile_cols == jnp.arange(blocks_wide, dtype=jnp.int32)[None, :]
    return (counts, row_mask, col_mask)


def dense_product(dense_block, b_columns):
    return lax.dot_general(
        dense_block, b_columns, (((0,), (0,)), ((), ())), preferred_element_type=jnp.float32
    )


def dense_builder(tile_values, tile_counts, tile_cols):
    slots = tile_values.shape[0]
    edge = tile_values.shape[1]
    blocks_tall = tile_counts.shape[0]
    counts, row_mask, col_mask = selection(tile_counts, tile_cols, slots, BC_DEV)
    selector = (row_mask[:, :, None] & col_mask[:, None, :]).astype(jnp.bfloat16)
    dense_block = jnp.einsum(
        "sij,sab->iajb", selector, tile_values, preferred_element_type=jnp.float32
    )
    dense_block = dense_block.astype(jnp.bfloat16).reshape(blocks_tall * edge, BC_DEV * edge)

    def tile_term(b_columns, flipped):
        return dense_product(dense_block, b_columns)

    return tile_term


def per_device(tile_values, tile_counts, tile_cols, panels):
    tile_term = dense_builder(tile_values, tile_counts, tile_cols)
    partial_value = tile_term(lax.all_gather(panels, "col", axis=1, tiled=True), False)
    result = lax.psum_scatter(partial_value, "row", scatter_dimension=1, tiled=True)
    return result.astype(jnp.bfloat16)


def solution(mesh):
    return jax.shard_map(
        per_device,
        mesh=mesh,
        in_specs=(P("row", "col", None), P("row", "col"), P("row", "col"), P("row", "col")),
        out_specs=P("col", "row"),
        check_vma=False,
    )
```

profile of v0, /device:TPU:0, one launch (start us, length us, event | category | flops | bytes accessed | tf_op | source)
XLA Modules:
  0.0 200.9 jit_solution(5213519928399133125)
XLA Ops:
  6.5 0.0 all-gather.2.cloned.1.call-start
  6.5 0.7 all-gather.2.cloned.1.call-update
  7.3 0.0 reduce-scatter.2.cloned.1.call-start
  7.3 0.8 reduce-window.7
  8.1 0.7 iota_compare_fusion.2
  8.8 0.7 bitcast_subtract_fusion
  9.5 0.1 fusion.8
  9.5 1.8 fusion
  11.4 0.8 copy.7
  12.2 81.5 %all-gather.2.cloned.1.call-done = bf16[1536,4096]{1,0:T(8,128)(2,1)} async-done(((bf16[1536,1024]{1,0:T(8,128)(2,1)}), bf16[1536,4096]{1,0:T(8,128)(2,1)}) %all-gather.2.cloned.1.call-update) | async-done | bytes 12582928 | tf_op jit(solution)/shard_map/all_gather | solution.py:43
  93.7 9.6 %fusion.1 = f32[256,4096]{1,0:T(8,128)} fusion(bf16[1536,4096]{1,0:T(8,128)(2,1)} %all-gather.2.cloned.1.call-done, bf16[192,8,2,128]{3,2,1,0:T(2,128)(2,1)S(1)} %bitcast.21), kind=kOutput, calls=%fused_computation.2 | convolution fusion | flops 3221225472 | bytes 17563648 | tf_op jit(solution)/shard_map/dot_general | solution.py:19
  103.3 0.0 reduce-scatter.2.cloned.1.call-update
  103.3 88.9 %reduce-scatter.2.cloned.1.call-done = f32[256,512]{1,0:T(8,128)} async-done(((f32[256,4096]{1,0:T(8,128)}), f32[256,512]{1,0:T(8,128)}) %reduce-scatter.2.cloned.1.call-update) | async-done | bytes 524304 | tf_op jit(solution)/shard_map/reduce_scatter | solution.py:44
  192.2 1.8 convert_element_type.12
Async XLA Ops:
  6.5 87.2 %all-gather.2.cloned.1.call-start = ((), (), s32[]{:S(2)}) async-start(), calls=%async_computation.1 | async-start | bytes 15728640 | tf_op jit(solution)/shard_map/all_gather | solution.py:43
  7.3 185.0 %reduce-scatter.2.cloned.1.call-start = ((), (), s32[]{:S(2)}) async-start(), calls=%async_computation.2 | async-start | bytes 4718592 | tf_op jit(solution)/shard_map/reduce_scatter | solution.py:44
Sparse Core Ops, SparseCore 0:
  8.9 84.7 all-gather.1
  103.4 88.7 reduce-scatter.1
where the time goes:
time: 201 us
  waiting for transfers between devices  171 us (85%)
  between operations  13.4 us (7%)
  matrix products  11.4 us (6%)
  other arithmetic  4.01 us (2%)
    reduce_scatter x1, waiting for transfers between devices, per_device(): lax.psum_scatter(partial_value, 'row', scatter_dimension=1, tiled=True)  88.9 us
    all_gather x1, waiting for transfers between devices, per_device(): lax.all_gather(panels, 'col', axis=1, tiled=True)  81.5 us
    dot_general x1, matrix products, dense_product(): lax.dot_general(dense_block, b_columns, (((0,), (0,)), ((), ())), preferr...  9.57 us
  transfers between devices with their start and end apart: 2, of which 2 were waited for; matrix products, arithmetic and copies ran while one was open for 2% of the time, Pallas kernels for 0%

commit v1 on v0

v1 whole, which is shorter than its diff:
```python
import functools

import jax
import jax.numpy as jnp
from jax import lax
from jax.experimental import pallas as pl
from jax.experimental.pallas import tpu as pltpu
from jax.sharding import PartitionSpec as P

BC_DEV = 2
PAIR = 2
AHEAD = 4
MESH = pl.DeviceIdType.MESH


def build_dense(counts_ref, cols_ref, tiles_ref, at_ref):
    slots, tile, _ = tiles_ref.shape
    start = jnp.int32(0)
    for i in range(counts_ref.shape[0]):
        count = counts_ref[i, 0]
        here = jnp.minimum(start, slots - 1)
        after = jnp.minimum(start + 1, slots - 1)
        for j in range(BC_DEV):
            one = (count > 0) & (cols_ref[here, 0] == j)
            two = (count > 1) & (cols_ref[after, 0] == j)
            block = tiles_ref[jnp.where(two, after, here)]
            keep = jnp.where(one | two, 1.0, 0.0).astype(jnp.float32)
            block = (block.astype(jnp.float32) * keep).T.astype(jnp.bfloat16)
            at_ref[2 * j, :, i * tile : (i + 1) * tile] = block
        start = start + count


def kernel(
    n_row, n_col, counts_ref, cols_ref, tiles_ref, b_ref, o_ref,
    at_ref, own_ref, xs_ref, xr_ref, zup_ref, zdn_ref, fin_ref, land_ref,
    at_send, at_recv, fw_send, x_send, x_recv, z_send, up_recv, dn_recv, f_send, f_recv,
):
    row, col = lax.axis_index("row"), lax.axis_index("col")
    n_z, n_y = n_row // PAIR, n_col // PAIR
    chunks = 2 * n_col
    z, x = row // PAIR, lax.rem(row, PAIR)
    y, k = col // PAIR, lax.rem(col, PAIR)
    wide = b_ref.shape[1] // PAIR

    def row_of(z_at, x_at):
        return z_at * PAIR + x_at

    def col_of(y_at, k_at):
        return y_at * PAIR + k_at

    beside = (row_of(z, 1 - x), col)
    above = (row_of(lax.rem(z + 1, n_z), x), col)
    below = (row_of(lax.rem(z + n_z - 1, n_z), x), col)
    partner = (row, col_of(y, 1 - k))

    barrier = pltpu.get_barrier_semaphore()
    for other in (beside, above, below):
        pl.semaphore_signal(barrier, inc=1, device_id=other, device_id_type=MESH)
    for step in range(1, n_col):
        pl.semaphore_signal(
            barrier, inc=1, device_id=(row, lax.rem(col + step, n_col)), device_id_type=MESH
        )
    build_dense(counts_ref, cols_ref, tiles_ref, at_ref)
    pl.semaphore_wait(barrier, 3 + n_col - 1)

    def copy(src, dst, send, recv, device):
        return pltpu.make_async_remote_copy(
            src_ref=src, dst_ref=dst, send_sem=send, recv_sem=recv,
            device_id=device, device_id_type=MESH,
        )

    first = []
    for j in range(BC_DEV):
        first.append(copy(at_ref.at[2 * j], at_ref.at[2 * j + 1], at_send.at[j],
                          at_recv.at[2 * j + 1], partner))
        for dy in range(1, n_y):
            to = (row, col_of(lax.rem(y + n_y - dy, n_y), k))
            slot = dy * 4 + 2 * j
            first.append(copy(at_ref.at[2 * j], at_ref.at[slot], at_send.at[dy * 2 + j],
                              at_recv.at[slot], to))
    for c in first:
        c.start()

    def forward(i):
        return copy(at_ref.at[i], at_ref.at[i + 1], fw_send.at[i], at_recv.at[i + 1], partner)

    def x_copy(i):
        return copy(xs_ref.at[i], xr_ref.at[i], x_send.at[i], x_recv.at[i], beside)

    def down_copy(i):
        return copy(own_ref.at[i], zup_ref.at[i], z_send.at[i], up_recv.at[i], below)

    def up_copy(i):
        return copy(own_ref.at[i], zdn_ref.at[i], z_send.at[i], dn_recv.at[i], above)

    def owner(i):
        dy, kk = i // 4, lax.rem(i, 2)
        return (row, col_of(lax.rem(y + dy, n_y), lax.rem(k + kk, PAIR)))

    def fin_copy(i):
        j = lax.rem(i, 4) // 2
        return copy(fin_ref.at[i], land_ref.at[j], f_send.at[i], f_recv.at[j], owner(i))

    def mine(i):
        return (i // 4 == 0) & (lax.rem(i, 2) == 0)

    def compute(i):
        @pl.when(jnp.logical_not(mine(i)))
        def _():
            copy(at_ref.at[i], at_ref.at[i], fw_send.at[i], at_recv.at[i], partner).wait_recv()

        @pl.when((i // 4 > 0) & (lax.rem(i, 2) == 0))
        def _():
            forward(i).start()

        lhs = at_ref[i]
        away = pl.ds(pl.multiple_of((1 - x) * wide, wide), wide)
        xs_ref[i] = jnp.dot(lhs, b_ref[:, away], preferred_element_type=jnp.float32)
        x_copy(i).start()
        here = pl.ds(pl.multiple_of(x * wide, wide), wide)
        own_ref[i] = jnp.dot(lhs, b_ref[:, here], preferred_element_type=jnp.float32)

    final = z == col

    def combine(i):
        x_copy(i).wait_recv()
        own_ref[i] += xr_ref[i]

        @pl.when((z >= col) & (z < n_z - 1))
        def _():
            down_copy(i).wait_recv()
            own_ref[i] += zup_ref[i]

        @pl.when((z <= col) & (z > 0))
        def _():
            up_copy(i).wait_recv()
            own_ref[i] += zdn_ref[i]

        @pl.when(z > col)
        def _():
            down_copy(i).start()

        @pl.when(z < col)
        def _():
            up_copy(i).start()

        @pl.when(final)
        def _():
            fin_ref[i] = own_ref[i].astype(jnp.bfloat16)

            @pl.when(jnp.logical_not(mine(i)))
            def _():
                fin_copy(i).start()

    def lead(i, carry):
        compute(i)
        return carry

    lax.fori_loop(0, AHEAD, lead, 0)

    def main(i, carry):
        combine(i)

        @pl.when(i + AHEAD < chunks)
        def _():
            compute(i + AHEAD)

        return carry

    lax.fori_loop(0, chunks, main, 0)

    rows = land_ref.shape[1]
    for j in range(BC_DEV):
        @pl.when(final)
        def _(j=j):
            o_ref[j * rows : (j + 1) * rows] = fin_ref[2 * j]

        @pl.when(jnp.logical_not(final))
        def _(j=j):
            copy(fin_ref.at[2 * j], land_ref.at[j], f_send.at[2 * j], f_recv.at[j],
                 partner).wait_recv()
            o_ref[j * rows : (j + 1) * rows] = land_ref[j]

    for c in first:
        c.wait_send()

    def drain(i, carry):
        x_copy(i).wait_send()

        @pl.when((i // 4 > 0) & (lax.rem(i, 2) == 0))
        def _():
            forward(i).wait_send()

        @pl.when(jnp.logical_not(final))
        def _():
            down_copy(i).wait_send()

        @pl.when(final & jnp.logical_not(mine(i)))
        def _():
            fin_copy(i).wait_send()

        return carry

    lax.fori_loop(0, chunks, drain, 0)


def per_device(n_row, n_col, tile_values, tile_counts, tile_cols, panels):
    tile = tile_values.shape[1]
    deep, columns = panels.shape
    wide = columns // PAIR
    chunks = BC_DEV * n_col
    f32, bf16 = jnp.float32, jnp.bfloat16
    vmem = pl.BlockSpec(memory_space=pltpu.VMEM)
    smem = pl.BlockSpec(memory_space=pltpu.SMEM)
    dma = pltpu.SemaphoreType.DMA
    return pl.pallas_call(
        functools.partial(kernel, n_row, n_col),
        out_shape=jax.ShapeDtypeStruct((BC_DEV * tile, wide), bf16),
        in_specs=[smem, smem, vmem, vmem],
        out_specs=vmem,
        scratch_shapes=[
            pltpu.VMEM((chunks, tile, deep), bf16),
            pltpu.VMEM((chunks, tile, wide), f32),
            pltpu.VMEM((chunks, tile, wide), f32),
            pltpu.VMEM((chunks, tile, wide), f32),
            pltpu.VMEM((chunks, tile, wide), f32),
            pltpu.VMEM((chunks, tile, wide), f32),
            pltpu.VMEM((chunks, tile, wide), bf16),
            pltpu.VMEM((BC_DEV, tile, wide), bf16),
            dma((n_col,)),
            dma((chunks,)),
            dma((chunks,)),
            dma((chunks,)),
            dma((chunks,)),
            dma((chunks,)),
            dma((chunks,)),
            dma((chunks,)),
            dma((chunks,)),
            dma((BC_DEV,)),
        ],
        compiler_params=pltpu.CompilerParams(
            collective_id=0, has_side_effects=True, vmem_limit_bytes=56 * 1024 * 1024
        ),
    )(tile_counts, tile_cols, tile_values, panels)


def solution(mesh):
    n_row, n_col = mesh.shape["row"], mesh.shape["col"]
    return jax.shard_map(
        functools.partial(per_device, n_row, n_col),
        mesh=mesh,
        in_specs=(P("row", "col", None), P("row", "col"), P("row", "col"), P("row", "col")),
        out_specs=P("col", "row"),
        check_vma=False,
    )
```

time: 201 us -> 82.1 us (0.41)
  waiting for transfers between devices: 171 us -> 0 us
  Pallas kernels: 0 us -> 77.6 us
  between operations: 13.4 us -> 0.01 us
  matrix products: 11.4 us -> 0 us
  other arithmetic: 4.01 us -> 0 us
  local copies, waits for them, and re-layouts: 0.81 us -> 4.33 us
    reduce_scatter x1 -> x0, waiting for transfers between devices: 88.9 us -> none  [per_device(): lax.psum_scatter(partial_value, 'row', scatter_dimension=1, tiled=True)]
    all_gather x1 -> x0, waiting for transfers between devices: 81.5 us -> none  [per_device(): lax.all_gather(panels, 'col', axis=1, tiled=True)]
    pallas_call x0 -> x1, Pallas kernels: none -> 77.6 us  [per_device(): pl.pallas_call(functools.partial(kernel, n_row, n_col), out_shape=jax.Sha...]
    dot_general x2 -> x0, matrix products: 11.4 us -> none  [the longest x1 9.57 us: dense_product(): lax.dot_general(dense_block, b_columns, (((0,), (0,)), ((), ())), preferr...]
    unnamed x0 -> x3, local copies, waits for them, and re-layouts: none -> 4.33 us
  transfers between devices with their start and end apart: 2 -> 0, of which waited for: 2 -> 0; matrix products, arithmetic and copies ran while one was open for 2% -> 0% of each run, Pallas kernels for 0% -> 0%
where the time goes in v1:
time: 82.1 us; the launch traced here: 81.9 us
  Pallas kernels  77.6 us (95%)
  local copies, waits for them, and re-layouts  4.33 us (5%)
    pallas_call x1, Pallas kernels, per_device(): pl.pallas_call(functools.partial(kernel, n_row, n_col), out_shape=jax.Sha...  77.6 us
    unnamed x3, local copies, waits for them, and re-layouts  4.33 us

profile of v1, /device:TPU:0, one launch (start us, length us, event | category | flops | bytes accessed | tf_op | source)
XLA Modules:
  0.0 81.9 jit_solution(5972214626566745407)
XLA Ops:
  0.0 1.3 %copy.5.counts_ref = s32[12,1]{1,0:T(8,128)} copy(s32[12,1]{0,1:T(1,128)} %param.5) | data formatting | bytes 96 | tf_op args[1]
  1.3 1.3 %copy.6.cols_ref = s32[24,1]{1,0:T(8,128)} copy(s32[24,1]{0,1:T(1,128)} %param.6) | data formatting | bytes 192 | tf_op args[2]
  2.7 77.6 %shard_map.46 = bf16[256,512]{1,0:T(8,128)(2,1)} custom-call(s32[12,1]{1,0:T(8,128)} %copy.5.counts_ref, s32[24,1]{1,0:T(8,128)} %copy.6.cols_ref, bf16[24,128,128]{2,1,0:T(8,128)(2,1)} %tiles_ref.1, bf16[1536,1024]{1,0:T(8,128)(2,1)} %b_ref.1), custom_call_target="tpu_custom_call" | custom-call | tf_op jit(solution)/shard_map/pallas_call | solution.py:216
  80.2 1.7 %copy.8 = bf16[256,512]{1,0:T(8,128)(2,1)} copy(bf16[256,512]{1,0:T(8,128)(2,1)} %shard_map.46) | data formatting | bytes 524288

commit v2 on v1

--- a/solution.py
+++ b/solution.py
@@ -9,20 +9,32 @@
 
 BC_DEV = 2
 PAIR = 2
-AHEAD = 4
+BEHIND = 3
+TOP = 32767.0
 MESH = pl.DeviceIdType.MESH
+
+
+def encode(value_ref, code_ref, step_ref):
+    value = value_ref[...]
+    peak = jnp.maximum(jnp.max(jnp.abs(value), axis=0, keepdims=True), 1e-30)
+    code_ref[...] = jnp.round(value * (TOP / peak)).astype(jnp.int32).astype(jnp.int16)
+    step_ref[...] = peak * (1.0 / TOP)
+
+
+def decode(code_ref, step_ref):
+    return code_ref[...].astype(jnp.int32).astype(jnp.float32) * step_ref[...]
 
 
 def build_dense(counts_ref, cols_ref, tiles_ref, at_ref):
     slots, tile, _ = tiles_ref.shape
     start = jnp.int32(0)
-    for i in range(counts_ref.shape[0]):
-        count = counts_ref[i, 0]
+    for i in range(counts_ref.shape[1]):
+        count = counts_ref[0, i]
         here = jnp.minimum(start, slots - 1)
         after = jnp.minimum(start + 1, slots - 1)
         for j in range(BC_DEV):
-            one = (count > 0) & (cols_ref[here, 0] == j)
-            two = (count > 1) & (cols_ref[after, 0] == j)
+            one = (count > 0) & (cols_ref[0, here] == j)
+            two = (count > 1) & (cols_ref[0, after] == j)
             block = tiles_ref[jnp.where(two, after, here)]
             keep = jnp.where(one | two, 1.0, 0.0).astype(jnp.float32)
             block = (block.astype(jnp.float32) * keep).T.astype(jnp.bfloat16)
@@ -32,7 +44,7 @@
 
 def kernel(
     n_row, n_col, counts_ref, cols_ref, tiles_ref, b_ref, o_ref,
-    at_ref, own_ref, xs_ref, xr_ref, zup_ref, zdn_ref, fin_ref, land_ref,
+    at_ref, away_ref, total_ref, own_ref, xs, xr, zs, zup, zdn, fin_ref, land_ref,
     at_send, at_recv, fw_send, x_send, x_recv, z_send, up_recv, dn_recv, f_send, f_recv,
 ):
     row, col = lax.axis_index("row"), lax.axis_index("col")
@@ -84,14 +96,33 @@
     def forward(i):
         return copy(at_ref.at[i], at_ref.at[i + 1], fw_send.at[i], at_recv.at[i + 1], partner)
 
+    class Both:
+        def __init__(self, src, dst, send, recv, i, device):
+            self.parts = [
+                copy(src[t].at[i], dst[t].at[i], send.at[t, i], recv.at[t, i], device)
+                for t in range(2)
+            ]
+
+        def start(self):
+            for part in self.parts:
+                part.start()
+
+        def wait_send(self):
+            for part in self.parts:
+                part.wait_send()
+
+        def wait_recv(self):
+            for part in self.parts:
+                part.wait_recv()
+
     def x_copy(i):
-        return copy(xs_ref.at[i], xr_ref.at[i], x_send.at[i], x_recv.at[i], beside)
+        return Both(xs, xr, x_send, x_recv, i, beside)
 
     def down_copy(i):
-        return copy(own_ref.at[i], zup_ref.at[i], z_send.at[i], up_recv.at[i], below)
+        return Both(zs, zup, z_send, up_recv, i, below)
 
     def up_copy(i):
-        return copy(own_ref.at[i], zdn_ref.at[i], z_send.at[i], dn_recv.at[i], above)
+        return Both(zs, zdn, z_send, dn_recv, i, above)
 
     def owner(i):
         dy, kk = i // 4, lax.rem(i, 2)
@@ -115,7 +146,8 @@
 
         lhs = at_ref[i]
         away = pl.ds(pl.multiple_of((1 - x) * wide, wide), wide)
-        xs_ref[i] = jnp.dot(lhs, b_ref[:, away], preferred_element_type=jnp.float32)
+        away_ref[...] = jnp.dot(lhs, b_ref[:, away], preferred_element_type=jnp.float32)
+        encode(away_ref, xs[0].at[i], xs[1].at[i])
         x_copy(i).start()
         here = pl.ds(pl.multiple_of(x * wide, wide), wide)
         own_ref[i] = jnp.dot(lhs, b_ref[:, here], preferred_element_type=jnp.float32)
@@ -124,17 +156,21 @@
 
     def combine(i):
         x_copy(i).wait_recv()
-        own_ref[i] += xr_ref[i]
+        total_ref[...] = own_ref[i] + decode(xr[0].at[i], xr[1].at[i])
 
         @pl.when((z >= col) & (z < n_z - 1))
         def _():
             down_copy(i).wait_recv()
-            own_ref[i] += zup_ref[i]
+            total_ref[...] += decode(zup[0].at[i], zup[1].at[i])
 
         @pl.when((z <= col) & (z > 0))
         def _():
             up_copy(i).wait_recv()
-            own_ref[i] += zdn_ref[i]
+            total_ref[...] += decode(zdn[0].at[i], zdn[1].at[i])
+
+        @pl.when(jnp.logical_not(final))
+        def _():
+            encode(total_ref, zs[0].at[i], zs[1].at[i])
 
         @pl.when(z > col)
         def _():
@@ -146,28 +182,24 @@
 
         @pl.when(final)
         def _():
-            fin_ref[i] = own_ref[i].astype(jnp.bfloat16)
+            fin_ref[i] = total_ref[...].astype(jnp.bfloat16)
 
             @pl.when(jnp.logical_not(mine(i)))
             def _():
                 fin_copy(i).start()
 
-    def lead(i, carry):
-        compute(i)
+    def main(i, carry):
+        @pl.when(i < chunks)
+        def _():
+            compute(i)
+
+        @pl.when(i >= BEHIND)
+        def _():
+            combine(i - BEHIND)
+
         return carry
 
-    lax.fori_loop(0, AHEAD, lead, 0)
-
-    def main(i, carry):
-        combine(i)
-
-        @pl.when(i + AHEAD < chunks)
-        def _():
-            compute(i + AHEAD)
-
-        return carry
-
-    lax.fori_loop(0, chunks, main, 0)
+    lax.fori_loop(0, chunks + BEHIND, main, 0)
 
     rows = land_ref.shape[1]
     for j in range(BC_DEV):
@@ -213,6 +245,7 @@
     vmem = pl.BlockSpec(memory_space=pltpu.VMEM)
     smem = pl.BlockSpec(memory_space=pltpu.SMEM)
     dma = pltpu.SemaphoreType.DMA
+    coded = (pltpu.VMEM((chunks, tile, wide), jnp.int16), pltpu.VMEM((chunks, 1, wide), f32))
     return pl.pallas_call(
         functools.partial(kernel, n_row, n_col),
         out_shape=jax.ShapeDtypeStruct((BC_DEV * tile, wide), bf16),
@@ -220,28 +253,31 @@
         out_specs=vmem,
         scratch_shapes=[
             pltpu.VMEM((chunks, tile, deep), bf16),
+            pltpu.VMEM((tile, wide), f32),
+            pltpu.VMEM((tile, wide), f32),
             pltpu.VMEM((chunks, tile, wide), f32),
-            pltpu.VMEM((chunks, tile, wide), f32),
-            pltpu.VMEM((chunks, tile, wide), f32),
-            pltpu.VMEM((chunks, tile, wide), f32),
-            pltpu.VMEM((chunks, tile, wide), f32),
+            coded,
+            coded,
+            coded,
+            coded,
+            coded,
             pltpu.VMEM((chunks, tile, wide), bf16),
             pltpu.VMEM((BC_DEV, tile, wide), bf16),
             dma((n_col,)),
             dma((chunks,)),
             dma((chunks,)),
-            dma((chunks,)),
-            dma((chunks,)),
-            dma((chunks,)),
-            dma((chunks,)),
-            dma((chunks,)),
+            dma((2, chunks)),
+            dma((2, chunks)),
+            dma((2, chunks)),
+            dma((2, chunks)),
+            dma((2, chunks)),
             dma((chunks,)),
             dma((BC_DEV,)),
         ],
         compiler_params=pltpu.CompilerParams(
             collective_id=0, has_side_effects=True, vmem_limit_bytes=56 * 1024 * 1024
         ),
-    )(tile_counts, tile_cols, tile_values, panels)
+    )(tile_counts.T, tile_cols.T, tile_values, panels)
 
 
 def solution(mesh):

time: 82.1 us -> 56.6 us (0.69)
  Pallas kernels: 77.6 us -> 54.8 us
  local copies, waits for them, and re-layouts: 4.33 us -> 1.67 us
    pallas_call x1, Pallas kernels: 77.6 us -> 54.8 us  [per_device(): pl.pallas_call(functools.partial(kernel, n_row, n_col), out_shape=jax.Sha...]
    unnamed x3 -> x1, local copies, waits for them, and re-layouts: 4.33 us -> 1.67 us
where the time goes in v2:
time: 56.6 us; the launch traced here: 56.5 us
  Pallas kernels  54.8 us (97%)
  local copies, waits for them, and re-layouts  1.67 us (3%)
    pallas_call x1, Pallas kernels, per_device(): pl.pallas_call(functools.partial(kernel, n_row, n_col), out_shape=jax.Sha...  54.8 us
    unnamed x1, local copies, waits for them, and re-layouts  1.67 us

profile of v2, /device:TPU:0, one launch (start us, length us, event | category | flops | bytes accessed | tf_op | source)
XLA Modules:
  0.0 56.5 jit_solution(9364735625534600862)
XLA Ops:
  0.0 54.8 %shard_map.46 = bf16[256,512]{1,0:T(8,128)(2,1)} custom-call(s32[1,12]{1,0:T(1,128)} %bitcast.2, s32[1,24]{1,0:T(1,128)} %bitcast.3, bf16[24,128,128]{2,1,0:T(8,128)(2,1)} %tiles_ref.1, bf16[1536,1024]{1,0:T(8,128)(2,1)} %b_ref.1), custom_call_target="tpu_custom_call" | custom-call | tf_op jit(solution)/shard_map/pallas_call | solution.py:249
  54.8 1.7 %copy.6 = bf16[256,512]{1,0:T(8,128)(2,1)} copy(bf16[256,512]{1,0:T(8,128)(2,1)} %shard_map.46) | data formatting | bytes 524288

commit v3 on v2

--- a/solution.py
+++ b/solution.py
@@ -9,7 +9,7 @@
 
 BC_DEV = 2
 PAIR = 2
-BEHIND = 3
+BEHIND = 2
 TOP = 32767.0
 MESH = pl.DeviceIdType.MESH
 

time: 56.6 us -> 53.8 us (0.951)
  Pallas kernels: 54.8 us -> 52 us
    pallas_call x1, Pallas kernels: 54.8 us -> 52 us  [per_device(): pl.pallas_call(functools.partial(kernel, n_row, n_col), out_shape=jax.Sha...]
where the time goes in v3:
time: 53.8 us; the launch traced here: 53.6 us
  Pallas kernels  52 us (97%)
  local copies, waits for them, and re-layouts  1.67 us (3%)
    pallas_call x1, Pallas kernels, per_device(): pl.pallas_call(functools.partial(kernel, n_row, n_col), out_shape=jax.Sha...  52 us
    unnamed x1, local copies, waits for them, and re-layouts  1.67 us

profile of v3, /device:TPU:0, one launch (start us, length us, event | category | flops | bytes accessed | tf_op | source)
XLA Modules:
  0.0 53.6 jit_solution(2722554405306054197)
XLA Ops:
  0.0 52.0 %shard_map.46 = bf16[256,512]{1,0:T(8,128)(2,1)} custom-call(s32[1,12]{1,0:T(1,128)} %bitcast.2, s32[1,24]{1,0:T(1,128)} %bitcast.3, bf16[24,128,128]{2,1,0:T(8,128)(2,1)} %tiles_ref.1, bf16[1536,1024]{1,0:T(8,128)(2,1)} %b_ref.1), custom_call_target="tpu_custom_call" | custom-call | tf_op jit(solution)/shard_map/pallas_call | solution.py:249
  52.0 1.7 %copy.6 = bf16[256,512]{1,0:T(8,128)(2,1)} copy(bf16[256,512]{1,0:T(8,128)(2,1)} %shard_map.46) | data formatting | bytes 524288
